TPU v7x, 32 devices: a whole 2x2x4 slice. The times are simulated.
32 devices in a mesh: grp: 4 (over y, x), dev: 8 (over z, core).
Axes of the slice: x: 2, y: 2, z: 4, core: 2. Of those that a mesh axis runs over, the one named last changes fastest.
Arguments:
- obs_coord: float32 [3, 131072], P(None, ('grp', 'dev')), may hold values from -1 to 1
- obs_resid: float32 [131072], P(('grp', 'dev')), may hold values from -6 to 6
- obs_weight: float32 [131072], P(('grp', 'dev')), may hold values from 0.5 to 2
- obs_dest: int32 [131072], P(('grp', 'dev')), may hold values from 0 to 7, as said below
- obs_send_slot: int32 [131072], P(('grp', 'dev')), may hold values from 0 to 1023, as said below
- obs_elem: int32 [131072], P(('grp', 'dev')), may hold values from 0 to 255, as said below
- obs_slot: int32 [131072], P(('grp', 'dev')), may hold values from 0 to 31, as said below
Outputs:
- nodal: float32 [16, 64, 8, 512], P('grp', 'dev')
- total_cost: float32 [], replicated
Inputs may be any that keep to these rules, and one draw needn't show every extreme that they name: `obs_dest`: from the rows of one device, at most 1024 observations go to any one destination; in every group one destination receives exactly 1024 from every device of the group. `obs_send_slot`: distinct among the rows of one device with the same obs_dest. `obs_elem`: together with obs_slot distinct among all observations of a group with the same obs_dest. `obs_slot`: on every destination some element uses all 32 slots.
All inputs are finite; a program needn't handle non-finite values.
Results may differ from a plain program's by a relative error of at most 0.00017.
Values sent between devices are 32-bit elements; how exact they have to be, the bound alone decides.
A program may use at most 64 MiB of HBM per device.

v0:
```python
import math
import jax
import jax.numpy as jnp
from jax import lax
from jax.sharding import PartitionSpec as P

EX = 4
EY = 8
EZ = 8
ELEM_DEV = 256
SLOTS = 32


def with_halo(block, sides, width):
    for axis, dim in sides:
        count = lax.axis_size(axis)
        forward = [(i, i + 1) for i in range(count - 1)]
        backward = [(target, source) for source, target in forward]
        low = lax.ppermute(
            lax.slice_in_dim(block, block.shape[dim] - width, None, axis=dim), axis, forward
        )
        high = lax.ppermute(lax.slice_in_dim(block, 0, width, axis=dim), axis, backward)
        block = jnp.concatenate([low, block, high], axis=dim)
    return block


def basis_values(position):
    anchors = [-math.cos(math.pi * k / 7) for k in range(8)]
    basis = []
    for node_i in range(8):
        factor = jnp.ones_like(position)
        for node_m in range(8):
            if node_m != node_i:
                factor = factor * (
                    (position - anchors[node_m]) / (anchors[node_i] - anchors[node_m])
                )
        basis.append(factor)
    return jnp.stack(basis)


def contract(first_w, second_w, third_w):
    outer = (first_w[:, None, :] * second_w[None, :, :]).reshape(64, ELEM_DEV, SLOTS)
    third = third_w.reshape(8, ELEM_DEV, SLOTS)
    mixed = jnp.einsum("aes,kes->eak", outer, third, precision=lax.Precision.HIGHEST)
    return mixed.reshape(ELEM_DEV, 512)


def combine(field, elem_dim, node_dim, from_low, from_high):
    count = field.shape[elem_dim]
    low_plane = lax.slice_in_dim(field, 0, 1, axis=node_dim)
    high_plane = lax.slice_in_dim(field, 7, 8, axis=node_dim)
    after = jnp.concatenate(
        [lax.slice_in_dim(low_plane, 1, count, axis=elem_dim), from_high], axis=elem_dim
    )
    before = jnp.concatenate(
        [from_low, lax.slice_in_dim(high_plane, 0, count - 1, axis=elem_dim)], axis=elem_dim
    )
    middle = lax.slice_in_dim(field, 1, 7, axis=node_dim)
    return jnp.concatenate([low_plane + before, middle, high_plane + after], axis=node_dim)


def boundary(field, elem_dim, node_dim):
    count = field.shape[elem_dim]
    low_plane = lax.slice_in_dim(field, 0, 1, axis=node_dim)
    high_plane = lax.slice_in_dim(field, 7, 8, axis=node_dim)
    return jnp.concatenate(
        [
            lax.slice_in_dim(low_plane, 0, 1, axis=elem_dim),
            lax.slice_in_dim(high_plane, count - 1, count, axis=elem_dim),
        ],
        axis=elem_dim,
    )


def on_device(obs_coord, obs_resid, obs_weight, obs_dest, obs_send_slot, obs_elem, obs_slot):
    peer_count = lax.axis_size("dev")
    row_count = obs_resid.shape[0]
    capacity = 2 * row_count // peer_count
    cell_count = ELEM_DEV * SLOTS
    forcing = obs_weight * obs_resid
    total_cost = lax.psum(0.5 * jnp.sum(forcing * obs_resid), ("grp", "dev"))
    payload = jnp.concatenate([obs_coord, forcing[None, :]], axis=0)
    channels = payload.shape[0]
    target = obs_dest * capacity + obs_send_slot
    cell_ids = obs_elem * SLOTS + obs_slot
    send_values = (
        jnp.zeros((channels, peer_count * capacity), payload.dtype).at[:, target].set(payload)
    )
    send_cells = jnp.full((peer_count * capacity,), cell_count, jnp.int32).at[target].set(cell_ids)
    send_values = send_values.reshape(channels, peer_count, capacity)
    send_cells = send_cells.reshape(1, peer_count, capacity)
    got_values, got_cells = (
        lax.all_to_all(send_values, "dev", split_axis=1, concat_axis=1, tiled=True),
        lax.all_to_all(send_cells, "dev", split_axis=1, concat_axis=1, tiled=True),
    )
    packed = jnp.zeros((channels, cell_count + 1), payload.dtype)
    packed = packed.at[:, got_cells.reshape(-1)].set(got_values.reshape(channels, -1))[
        :, :cell_count
    ]
    first_w = basis_values(packed[0]) * packed[3]
    second_w = basis_values(packed[1])
    third_w = basis_values(packed[2])
    field = contract(first_w, second_w, third_w).reshape(EX, EY, EZ, 8, 8, 8)
    padded = with_halo(boundary(field, 0, 3), (("grp", 0),), 1)
    field = combine(field, 0, 3, padded[0:1], padded[3:4])
    padded = with_halo(boundary(field, 1, 4), (("dev", 1),), 1)
    field = combine(field, 1, 4, padded[:, 0:1], padded[:, 3:4])
    empty = jnp.zeros_like(lax.slice_in_dim(lax.slice_in_dim(field, 0, 1, axis=5), 0, 1, axis=2))
    field = combine(field, 2, 5, empty, empty)
    return (field.reshape(EX, EY, EZ, 512), total_cost)


def solution(mesh):
    placed = (
        P(None, ("grp", "dev")),
        P(("grp", "dev")),
        P(("grp", "dev")),
        P(("grp", "dev")),
        P(("grp", "dev")),
        P(("grp", "dev")),
        P(("grp", "dev")),
    )
    return jax.shard_map(
        on_device,
        mesh=mesh,
        in_specs=placed,
        out_specs=(P("grp", "dev", None, None), P()),
        check_vma=False,
    )
```

profile of v0, /device:TPU:1, one launch (start us, length us, event | category | flops | bytes accessed | tf_op | source)
XLA Modules:
  0.0 226.2 jit_solution(2030563538721729877)
XLA Ops:
  0.6 0.8 compare_select_fusion.1
  1.4 16.1 %scatter_custom_fusion = s32[8192]{0:T(1024)} fusion(s32[4096]{0:T(1024)S(1)} %get-tuple-element.54, s32[4096]{0:T(1024)S(1)} %get-tuple-element.55, s32[]{:T(128)} %constant.245.clone.1), kind=kCustom, calls=%fused_computation.88 | custom fusion | bytes 32772 | tf_op jit(solution)/shard_map/scatter | solution.py:89
  17.5 6.4 %all-to-all-start = ((s32[1,8,1024]{2,0,1:T(1,128)}), s32[1,8,1024]{2,0,1:T(1,128)S(1)}, u32[]{:S(2)}, u32[]{:S(2)}) async-start(s32[1,8,1024]{2,0,1:T(1,128)} %bitcast), calls=%async_computation | async-start | bytes 65536 | tf_op jit(solution)/shard_map/all_to_all | solution.py:94
  23.9 1.3 multiply_reduce_fusion.8
  25.9 0.9 maximum_bitcast_fusion
  26.7 39.5 %psum.7 = f32[]{:T(128)} all-reduce(f32[]{:T(128)S(6)} %mul_shard_map.3), channel_id=1, replica_groups=mesh['grp'=4,'dev'=8] {'grp','dev'}, use_global_device_ids=true, to_apply=%region_4.0 | all-reduce | flops 1 | bytes 8 | tf_op jit(solution)/shard_map/psum | solution.py:81
  66.2 0.6 copy.404
  66.9 12.8 %scatter_custom_fusion.1 = f32[4,8192]{0,1:T(8,128)} fusion(s32[4096]{0:T(1024)S(1)} %get-tuple-element.54, f32[4096,4]{1,0:T(8,128)S(1)} %copy.404, f32[]{:T(128)} %constant.244.clone.1), kind=kCustom, calls=%fused_computation.11 | custom fusion | bytes 131076 | tf_op jit(solution)/shard_map/scatter | solution.py:87
  79.6 3.5 %copy.405 = f32[4,8,1024]{2,0,1:T(4,128)} copy(f32[4,8,1024]{0,2,1:T(8,128)} %bitcast.26) | data formatting | bytes 262144 | tf_op jit(solution)/shard_map/reshape | solution.py:90
  83.1 0.0 all-to-all-done
  83.1 4.9 %all-to-all-start.1 = ((f32[4,8,1024]{2,0,1:T(4,128)}), f32[4,8,1024]{2,0,1:T(4,128)S(1)}, u32[]{:S(2)}, u32[]{:S(2)}) async-start(f32[4,8,1024]{2,0,1:T(4,128)} %copy.405), calls=%async_computation.1 | async-start | bytes 262144 | tf_op jit(solution)/shard_map/all_to_all | solution.py:93
  88.0 5.7 %all-to-all-done.1 = f32[4,8,1024]{2,0,1:T(4,128)S(1)} async-done(((f32[4,8,1024]{2,0,1:T(4,128)}), f32[4,8,1024]{2,0,1:T(4,128)S(1)}, u32[]{:S(2)}, u32[]{:S(2)}) %all-to-all-start.1) | async-done | bytes 131104 | tf_op jit(solution)/shard_map/all_to_all | solution.py:93
  93.7 2.6 %copy.406 = f32[8192,4]{1,0:T(8,128)} copy(f32[8192,4]{0,1:T(4,128)S(1)} %bitcast.35) | data formatting | bytes 262144 | tf_op jit(solution)/shard_map/reshape | solution.py:97
  96.4 23.0 %scatter_custom_fusion.2 = f32[4,8193]{0,1:T(8,128)} fusion(s32[8192]{0:T(1024)S(1)} %bitcast.38, f32[8192,4]{1,0:T(8,128)} %copy.406, f32[]{:T(128)} %constant.244.clone.1), kind=kCustom, calls=%fused_computation.9 | custom fusion | bytes 131600 | tf_op jit(solution)/shard_map/scatter | solution.py:97
  119.4 14.8 %slice_reduce_fusion = (f32[8192]{0:T(1024)S(1)}, f32[1,8192]{0,1:T(8,128)}, f32[1,8192]{0,1:T(8,128)}, f32[1,8192]{0,1:T(8,128)}) fusion(f32[4,8193]{0,1:T(8,128)} %scatter_custom_fusion.2), kind=kLoop, calls=%fused_computation.8 | loop fusion | bytes 262144 | tf_op jit(solution)/shard_map/slice | solution.py:100
  134.2 2.8 %copy.422 = f32[1,8192]{1,0:T(1,128)S(1)} copy(f32[1,8192]{0,1:T(8,128)} %get-tuple-element.35) | data formatting | bytes 65536
  137.0 2.8 %copy.421 = f32[1,8192]{1,0:T(1,128)S(1)} copy(f32[1,8192]{0,1:T(8,128)} %get-tuple-element.36) | data formatting | bytes 65536
  139.9 2.8 %copy.423 = f32[1,8192]{1,0:T(1,128)S(1)} copy(f32[1,8192]{0,1:T(8,128)} %get-tuple-element.37) | data formatting | bytes 65536
  142.7 1.9 multiply_reduce_fusion
  144.6 0.1 stack.58
  144.7 0.1 stack.57
  144.8 0.1 stack.56
  144.9 0.1 stack.55
  145.0 0.1 stack.54
  145.1 0.1 stack.26
  145.2 0.1 stack.25
  145.3 0.8 stack.24
  146.0 1.0 multiply_multiply_fusion.8
  147.0 1.0 multiply_multiply_fusion
  148.0 0.4 stack.22
  148.4 0.4 stack.23
  148.8 0.1 broadcast_multiply_fusion
  149.0 0.0 copy-start
  149.0 4.8 %mul.732 = f32[64,256,32]{2,1,0:T(8,128)} reshape(f32[8,8,8192]{2,1,0:T(8,128)S(1)} %broadcast_multiply_fusion) | data formatting | bytes 4194304 | tf_op jit(solution)/shard_map/mul | solution.py:42
  153.8 0.0 copy-done
  153.8 1.6 stack.59
  155.4 20.7 %fusion = f32[256,64,8]{1,2,0:T(8,128)S(1)} fusion(f32[8,256,32]{2,0,1:T(8,128)S(1)} %stack.59, f32[64,256,32]{2,1,0:T(8,128)} %mul.732), kind=kOutput, calls=%fused_computation.6 | convolution fusion | flops 50331648 | bytes 2883584 | tf_op jit(solution)/shard_map/aes,kes->eak/dot_general | solution.py:44
  176.1 0.5 copy.419
  176.5 6.2 %reshape_reshape.3 = f32[4,8,8,8,8,8]{2,1,0,5,4,3:T(8,128)} reshape(f32[256,64,8]{0,2,1:T(8,128)S(1)} %copy.419) | data formatting | bytes 1048576 | tf_op jit(solution)/shard_map/reshape;reshape | solution.py:103
  182.7 1.1 fusion.14
  183.8 3.9 %collective-permute-start = (f32[1,8,8,1,8,8]{2,1,0,5,4,3:T(8,128)S(1)}, f32[1,8,8,1,8,8]{2,1,0,5,4,3:T(8,128)S(1)}, u32[]{:S(2)}, u32[]{:S(2)}) collective-permute-start(f32[1,8,8,1,8,8]{2,1,0,5,4,3:T(8,128)S(1)} %get-tuple-element.30), channel_id=1, source_target_pairs={{0,8},{8,16},{16,24},{1,9},{9,17},{17,25},{2,10},{10,18},{18,26},{... | collective-permute-start | bytes 49160 | tf_op jit(solution)/shard_map/ppermute | solution.py:19
  187.7 1.3 collective-permute-start.1
  189.0 1.5 fusion.15
  190.5 3.5 %slice.118 = f32[4,8,8,6,8,8]{2,1,0,5,4,3:T(8,128)S(1)} slice(f32[4,8,8,8,8,8]{2,1,0,5,4,3:T(8,128)} %reshape_reshape.3), slice={[0:4], [0:8], [0:8], [1:7], [0:8], [0:8]} | slice | bytes 786432 | tf_op jit(solution)/shard_map/slice | solution.py:58
  194.0 0.0 collective-permute-done
  194.0 6.1 %collective-permute-done.1 = f32[1,8,8,1,8,8]{2,1,0,5,4,3:T(8,128)S(1)} collective-permute-done((f32[1,8,8,1,8,8]{2,1,0,5,4,3:T(8,128)S(1)}, f32[1,8,8,1,8,8]{2,1,0,5,4,3:T(8,128)S(1)}, u32[]{:S(2)}, u32[]{:S(2)}) %collective-permute-start.1) | collective-permute-done | bytes 16416 | tf_op jit(solution)/shard_map/ppermute | solution.py:22
  200.1 1.9 slice_add_fusion.1
  202.0 0.3 pad_maximum_fusion.8
  202.3 4.4 %collective-permute-start.2 = (f32[4,1,8,8,1,8]{2,1,0,5,4,3:T(1,128)S(1)}, f32[4,1,8,8,1,8]{2,1,0,5,4,3:T(1,128)S(1)}, u32[]{:S(2)}, u32[]{:S(2)}) collective-permute-start(f32[4,1,8,8,1,8]{2,1,0,5,4,3:T(1,128)S(1)} %get-tuple-element.26), channel_id=1, source_target_pairs={{0,1},{1,2},{2,3},{3,4},{4,5},{5,6},{6,7},{8,9},{9,10},{10,11},{11... | collective-permute-start | bytes 24584 | tf_op jit(solution)/shard_map/ppermute | solution.py:19
  206.7 1.9 collective-permute-start.3
  208.6 1.9 pad_maximum_fusion
  210.5 1.2 slice.122
  211.7 0.0 collective-permute-done.2
  211.8 1.2 collective-permute-done.3
  213.0 0.5 fusion.11
  213.5 0.6 fusion.7
  214.1 1.6 pad_maximum_fusion.1
  215.8 0.8 slice.123
  216.6 3.7 %pad_maximum_fusion.2 = f32[4,8,8,8,8,8]{2,1,0,5,4,3:T(8,128)} fusion(f32[4,8,8,8,8,1]{2,1,0,5,4,3:T(8,128)S(1)} %get-tuple-element.23, f32[4,8,8,8,8,6]{2,1,0,5,4,3:T(8,128)S(1)} %slice.123, f32[4,8,8,8,8,1]{2,1,0,5,4,3:T(8,128)S(1)} %get-tuple-element.22), kind=kLoop, calls=%fused_computation.5 | loop fusion | flops 262144 | bytes 1048576 | tf_op jit(solution)/shard_map/concatenate | solution.py:59
  220.3 5.9 %copy.420 = f32[4,8,8,512]{3,2,1,0:T(8,128)} copy(f32[4,8,8,512]{2,1,0,3:T(8,128)} %bitcast.25) | data formatting | bytes 1048576
  (2 shorter events, 0.1 us)
Async XLA Ops:
  17.5 65.6 %all-to-all-start = ((s32[1,8,1024]{2,0,1:T(1,128)}), s32[1,8,1024]{2,0,1:T(1,128)S(1)}, u32[]{:S(2)}, u32[]{:S(2)}) async-start(s32[1,8,1024]{2,0,1:T(1,128)} %bitcast), calls=%async_computation | async-start | bytes 65536 | tf_op jit(solution)/shard_map/all_to_all | solution.py:94
  83.1 10.6 %all-to-all-start.1 = ((f32[4,8,1024]{2,0,1:T(4,128)}), f32[4,8,1024]{2,0,1:T(4,128)S(1)}, u32[]{:S(2)}, u32[]{:S(2)}) async-start(f32[4,8,1024]{2,0,1:T(4,128)} %copy.405), calls=%async_computation.1 | async-start | bytes 262144 | tf_op jit(solution)/shard_map/all_to_all | solution.py:93
  149.0 4.8 %copy-start = (f32[1,256,32]{2,1,0:T(8,128)S(1)}, f32[1,256,32]{2,1,0:T(8,128)}, u32[]{:S(2)}) copy-start(f32[1,256,32]{2,1,0:T(8,128)} %stack.24) | copy-start | bytes 98308
  183.8 10.2 %collective-permute-start = (f32[1,8,8,1,8,8]{2,1,0,5,4,3:T(8,128)S(1)}, f32[1,8,8,1,8,8]{2,1,0,5,4,3:T(8,128)S(1)}, u32[]{:S(2)}, u32[]{:S(2)}) collective-permute-start(f32[1,8,8,1,8,8]{2,1,0,5,4,3:T(8,128)S(1)} %get-tuple-element.30), channel_id=1, source_target_pairs={{0,8},{8,16},{16,24},{1,9},{9,17},{17,25},{2,10},{10,18},{18,26},{... | collective-permute-start | bytes 49160 | tf_op jit(solution)/shard_map/ppermute | solution.py:19
  187.7 12.4 %collective-permute-start.1 = (f32[1,8,8,1,8,8]{2,1,0,5,4,3:T(8,128)S(1)}, f32[1,8,8,1,8,8]{2,1,0,5,4,3:T(8,128)S(1)}, u32[]{:S(2)}, u32[]{:S(2)}) collective-permute-start(f32[1,8,8,1,8,8]{2,1,0,5,4,3:T(8,128)S(1)} %get-tuple-element.31), channel_id=1, source_target_pairs={{8,0},{16,8},{24,16},{9,1},{17,9},{25,17},{10,2},{18,10},{26,18},{... | collective-permute-start | bytes 49160 | tf_op jit(solution)/shard_map/ppermute | solution.py:22
  202.3 9.4 %collective-permute-start.2 = (f32[4,1,8,8,1,8]{2,1,0,5,4,3:T(1,128)S(1)}, f32[4,1,8,8,1,8]{2,1,0,5,4,3:T(1,128)S(1)}, u32[]{:S(2)}, u32[]{:S(2)}) collective-permute-start(f32[4,1,8,8,1,8]{2,1,0,5,4,3:T(1,128)S(1)} %get-tuple-element.26), channel_id=1, source_target_pairs={{0,1},{1,2},{2,3},{3,4},{4,5},{5,6},{6,7},{8,9},{9,10},{10,11},{11... | collective-permute-start | bytes 24584 | tf_op jit(solution)/shard_map/ppermute | solution.py:19
  206.7 6.3 %collective-permute-start.3 = (f32[4,1,8,8,1,8]{2,1,0,5,4,3:T(1,128)S(1)}, f32[4,1,8,8,1,8]{2,1,0,5,4,3:T(1,128)S(1)}, u32[]{:S(2)}, u32[]{:S(2)}) collective-permute-start(f32[4,1,8,8,1,8]{2,1,0,5,4,3:T(1,128)S(1)} %get-tuple-element.27), channel_id=1, source_target_pairs={{1,0},{2,1},{3,2},{4,3},{5,4},{6,5},{7,6},{9,8},{10,9},{11,10},{12... | collective-permute-start | bytes 24584 | tf_op jit(solution)/shard_map/ppermute | solution.py:22
where the time goes:
time: 227 us; the launch traced here: 226 us
  local copies, waits for them, and re-layouts  111 us (49%)
  blocking collectives  39.5 us (17%)
  starting transfers between devices  22.7 us (10%)
  matrix products  20.7 us (9%)
  other arithmetic  17.6 us (8%)
  waiting for transfers between devices  13 us (6%)
    psum x1, blocking collectives, on_device(): total_cost = lax.psum(0.5 * jnp.sum(forcing * obs_resid), ('grp', 'dev'))  39.5 us
    scatter x1, local copies, waits for them, and re-layouts, on_device(): packed.at[:, got_cells.reshape(-1)].set(got_values.reshape(channels, -1))  23 us
    dot_general x1, matrix products, contract(): jnp.einsum('aes,kes->eak', outer, third, precision=lax.Precision.HIGHEST)  20.7 us
    scatter x1, local copies, waits for them, and re-layouts, on_device(): jnp.full((peer_count * capacity,), cell_count, jnp.int32).at[target]  16.1 us
    slice x1, local copies, waits for them, and re-layouts, on_device(): first_w = basis_values(packed[0]) * packed[3]  14.8 us
    unnamed x6, local copies, waits for them, and re-layouts  14.4 us
    scatter x1, local copies, waits for them, and re-layouts, on_device(): jnp.zeros((channels, peer_count * capacity), payload.dtype).at[:, target]  12.8 us
    ppermute x2, starting transfers between devices, with_halo(): lax.ppermute(lax.slice_in_dim(block, block.shape[dim] - width, None, axis...  8.28 us
  transfers between devices with their start and end apart: 6, of which 3 were waited for; matrix products, arithmetic and copies ran while one was open for 12% of the time, Pallas kernels for 0%

commit v1 on v0

--- a/solution.py
+++ b/solution.py
@@ -78,7 +78,9 @@
     capacity = 2 * row_count // peer_count
     cell_count = ELEM_DEV * SLOTS
     forcing = obs_weight * obs_resid
-    total_cost = lax.psum(0.5 * jnp.sum(forcing * obs_resid), ("grp", "dev"))
+    part = 0.5 * jnp.sum(forcing * obs_resid)
+    parts = lax.all_gather(part, ("grp", "dev"), axis=0, tiled=False)
+    total_cost = parts.sum(axis=0)
     payload = jnp.concatenate([obs_coord, forcing[None, :]], axis=0)
     channels = payload.shape[0]
     target = obs_dest * capacity + obs_send_slot

time: 227 us -> 228 us (level)
    psum x1 -> x0, blocking collectives: 39.5 us -> none  [on_device(): total_cost = lax.psum(0.5 * jnp.sum(forcing * obs_resid), ('grp', 'dev'))]
    unnamed x0 -> x1, blocking collectives: none -> 39.3 us
    unnamed x6 -> x8, local copies, waits for them, and re-layouts: 14.4 us -> 14.5 us
where the time goes in v1:
time: 228 us; the launch traced here: 227 us
  local copies, waits for them, and re-layouts  111 us (49%)
  blocking collectives  39.3 us (17%)
  starting transfers between devices  22.9 us (10%)
  matrix products  20.7 us (9%)
  other arithmetic  18.2 us (8%)
  waiting for transfers between devices  12.8 us (6%)
    unnamed x1, blocking collectives  39.3 us
    scatter x1, local copies, waits for them, and re-layouts, on_device(): packed.at[:, got_cells.reshape(-1)].set(got_values.reshape(channels, -1))  23 us
    dot_general x1, matrix products, contract(): jnp.einsum('aes,kes->eak', outer, third, precision=lax.Precision.HIGHEST)  20.7 us
    scatter x1, local copies, waits for them, and re-layouts, on_device(): jnp.full((peer_count * capacity,), cell_count, jnp.int32).at[target]  16.1 us
    slice x1, local copies, waits for them, and re-layouts, on_device(): first_w = basis_values(packed[0]) * packed[3]  14.8 us
    unnamed x8, local copies, waits for them, and re-layouts  14.5 us
    scatter x1, local copies, waits for them, and re-layouts, on_device(): jnp.zeros((channels, peer_count * capacity), payload.dtype).at[:, target]  12.8 us
    ppermute x2, starting transfers between devices, with_halo(): lax.ppermute(lax.slice_in_dim(block, block.shape[dim] - width, None, axis...  8.28 us
  transfers between devices with their start and end apart: 6, of which 3 were waited for; matrix products, arithmetic and copies ran while one was open for 12% of the time, Pallas kernels for 0%

profile of v1, /device:TPU:1, one launch (start us, length us, event | category | flops | bytes accessed | tf_op | source)
XLA Modules:
  0.0 226.7 jit_solution(345657072784228396)
XLA Ops:
  0.6 0.8 compare_select_fusion.1
  1.4 16.1 %scatter_custom_fusion = s32[8192]{0:T(1024)} fusion(s32[4096]{0:T(1024)S(1)} %get-tuple-element.54, s32[4096]{0:T(1024)S(1)} %get-tuple-element.55, s32[]{:T(128)} %constant.245.clone.1), kind=kCustom, calls=%fused_computation.88 | custom fusion | bytes 32772 | tf_op jit(solution)/shard_map/scatter | solution.py:91
  17.5 6.4 %all-to-all-start = ((s32[1,8,1024]{2,0,1:T(1,128)}), s32[1,8,1024]{2,0,1:T(1,128)S(1)}, u32[]{:S(2)}, u32[]{:S(2)}) async-start(s32[1,8,1024]{2,0,1:T(1,128)} %bitcast), calls=%async_computation | async-start | bytes 65536 | tf_op jit(solution)/shard_map/all_to_all | solution.py:96
  23.9 1.3 multiply_reduce_fusion.8
  25.9 0.1 dynamic-update-slice
  26.0 0.9 maximum_bitcast_fusion
  26.9 39.3 %all-reduce.2 = f32[32]{0:T(128)S(1)} all-reduce(f32[32]{0:T(128)S(1)} %dynamic-update-slice), channel_id=1, replica_groups=mesh['grp'=4,'dev'=8] {'grp','dev'}, use_global_device_ids=true, to_apply=%add.2 | all-reduce | flops 32 | bytes 256
  66.2 0.6 reduce_sum.19
  66.8 0.6 copy.404
  67.4 12.8 %scatter_custom_fusion.1 = f32[4,8192]{0,1:T(8,128)} fusion(s32[4096]{0:T(1024)S(1)} %get-tuple-element.54, f32[4096,4]{1,0:T(8,128)S(1)} %copy.404, f32[]{:T(128)} %constant.244.clone.1), kind=kCustom, calls=%fused_computation.11 | custom fusion | bytes 131076 | tf_op jit(solution)/shard_map/scatter | solution.py:89
  80.2 3.5 %copy.405 = f32[4,8,1024]{2,0,1:T(4,128)} copy(f32[4,8,1024]{0,2,1:T(8,128)} %bitcast.27) | data formatting | bytes 262144 | tf_op jit(solution)/shard_map/reshape | solution.py:92
  83.7 0.0 all-to-all-done
  83.7 5.0 %all-to-all-start.1 = ((f32[4,8,1024]{2,0,1:T(4,128)}), f32[4,8,1024]{2,0,1:T(4,128)S(1)}, u32[]{:S(2)}, u32[]{:S(2)}) async-start(f32[4,8,1024]{2,0,1:T(4,128)} %copy.405), calls=%async_computation.1 | async-start | bytes 262144 | tf_op jit(solution)/shard_map/all_to_all | solution.py:95
  88.7 5.7 %all-to-all-done.1 = f32[4,8,1024]{2,0,1:T(4,128)S(1)} async-done(((f32[4,8,1024]{2,0,1:T(4,128)}), f32[4,8,1024]{2,0,1:T(4,128)S(1)}, u32[]{:S(2)}, u32[]{:S(2)}) %all-to-all-start.1) | async-done | bytes 131104 | tf_op jit(solution)/shard_map/all_to_all | solution.py:95
  94.5 2.6 %copy.406 = f32[8192,4]{1,0:T(8,128)} copy(f32[8192,4]{0,1:T(4,128)S(1)} %bitcast.36) | data formatting | bytes 262144 | tf_op jit(solution)/shard_map/reshape | solution.py:99
  97.1 23.0 %scatter_custom_fusion.2 = f32[4,8193]{0,1:T(8,128)} fusion(s32[8192]{0:T(1024)S(1)} %bitcast.39, f32[8192,4]{1,0:T(8,128)} %copy.406, f32[]{:T(128)} %constant.244.clone.1), kind=kCustom, calls=%fused_computation.9 | custom fusion | bytes 131600 | tf_op jit(solution)/shard_map/scatter | solution.py:99
  120.1 14.8 %slice_reduce_fusion = (f32[8192]{0:T(1024)S(1)}, f32[1,8192]{0,1:T(8,128)}, f32[1,8192]{0,1:T(8,128)}, f32[1,8192]{0,1:T(8,128)}) fusion(f32[4,8193]{0,1:T(8,128)} %scatter_custom_fusion.2), kind=kLoop, calls=%fused_computation.8 | loop fusion | bytes 262144 | tf_op jit(solution)/shard_map/slice | solution.py:102
  134.9 2.8 %copy.422 = f32[1,8192]{1,0:T(1,128)S(1)} copy(f32[1,8192]{0,1:T(8,128)} %get-tuple-element.35) | data formatting | bytes 65536
  137.8 2.8 %copy.421 = f32[1,8192]{1,0:T(1,128)S(1)} copy(f32[1,8192]{0,1:T(8,128)} %get-tuple-element.36) | data formatting | bytes 65536
  140.6 2.8 %copy.423 = f32[1,8192]{1,0:T(1,128)S(1)} copy(f32[1,8192]{0,1:T(8,128)} %get-tuple-element.37) | data formatting | bytes 65536
  143.5 1.9 multiply_reduce_fusion
  145.4 0.1 stack.58
  145.4 0.1 stack.57
  145.5 0.1 stack.56
  145.6 0.1 stack.55
  145.7 0.1 stack.54
  145.8 0.1 stack.26
  145.9 0.1 stack.25
  146.0 0.8 stack.24
  146.8 1.0 multiply_multiply_fusion.8
  147.7 1.0 multiply_multiply_fusion
  148.7 0.4 stack.22
  149.2 0.4 stack.23
  149.5 0.1 broadcast_multiply_fusion
  149.7 0.0 copy-start
  149.7 4.8 %mul.732 = f32[64,256,32]{2,1,0:T(8,128)} reshape(f32[8,8,8192]{2,1,0:T(8,128)S(1)} %broadcast_multiply_fusion) | data formatting | bytes 4194304 | tf_op jit(solution)/shard_map/mul | solution.py:42
  154.5 0.0 copy-done
  154.5 1.6 stack.59
  156.1 20.7 %fusion = f32[256,64,8]{1,2,0:T(8,128)S(1)} fusion(f32[8,256,32]{2,0,1:T(8,128)S(1)} %stack.59, f32[64,256,32]{2,1,0:T(8,128)} %mul.732), kind=kOutput, calls=%fused_computation.6 | convolution fusion | flops 50331648 | bytes 2883584 | tf_op jit(solution)/shard_map/aes,kes->eak/dot_general | solution.py:44
  176.8 0.5 copy.419
  177.3 6.2 %reshape_reshape.3 = f32[4,8,8,8,8,8]{2,1,0,5,4,3:T(8,128)} reshape(f32[256,64,8]{0,2,1:T(8,128)S(1)} %copy.419) | data formatting | bytes 1048576 | tf_op jit(solution)/shard_map/reshape;reshape | solution.py:105
  183.4 1.1 fusion.14
  184.5 3.9 %collective-permute-start = (f32[1,8,8,1,8,8]{2,1,0,5,4,3:T(8,128)S(1)}, f32[1,8,8,1,8,8]{2,1,0,5,4,3:T(8,128)S(1)}, u32[]{:S(2)}, u32[]{:S(2)}) collective-permute-start(f32[1,8,8,1,8,8]{2,1,0,5,4,3:T(8,128)S(1)} %get-tuple-element.30), channel_id=1, source_target_pairs={{0,8},{8,16},{16,24},{1,9},{9,17},{17,25},{2,10},{10,18},{18,26},{... | collective-permute-start | bytes 49160 | tf_op jit(solution)/shard_map/ppermute | solution.py:19
  188.4 1.3 collective-permute-start.1
  189.7 1.5 fusion.15
  191.2 3.5 %slice.118 = f32[4,8,8,6,8,8]{2,1,0,5,4,3:T(8,128)S(1)} slice(f32[4,8,8,8,8,8]{2,1,0,5,4,3:T(8,128)} %reshape_reshape.3), slice={[0:4], [0:8], [0:8], [1:7], [0:8], [0:8]} | slice | bytes 786432 | tf_op jit(solution)/shard_map/slice | solution.py:58
  194.7 0.0 collective-permute-done
  194.7 5.9 %collective-permute-done.1 = f32[1,8,8,1,8,8]{2,1,0,5,4,3:T(8,128)S(1)} collective-permute-done((f32[1,8,8,1,8,8]{2,1,0,5,4,3:T(8,128)S(1)}, f32[1,8,8,1,8,8]{2,1,0,5,4,3:T(8,128)S(1)}, u32[]{:S(2)}, u32[]{:S(2)}) %collective-permute-start.1) | collective-permute-done | bytes 16416 | tf_op jit(solution)/shard_map/ppermute | solution.py:22
  200.6 1.9 slice_add_fusion.1
  202.5 0.3 pad_maximum_fusion.8
  202.9 4.4 %collective-permute-start.2 = (f32[4,1,8,8,1,8]{2,1,0,5,4,3:T(1,128)S(1)}, f32[4,1,8,8,1,8]{2,1,0,5,4,3:T(1,128)S(1)}, u32[]{:S(2)}, u32[]{:S(2)}) collective-permute-start(f32[4,1,8,8,1,8]{2,1,0,5,4,3:T(1,128)S(1)} %get-tuple-element.26), channel_id=1, source_target_pairs={{0,1},{1,2},{2,3},{3,4},{4,5},{5,6},{6,7},{8,9},{9,10},{10,11},{11... | collective-permute-start | bytes 24584 | tf_op jit(solution)/shard_map/ppermute | solution.py:19
  207.2 1.9 collective-permute-start.3
  209.1 1.9 pad_maximum_fusion
  211.0 1.2 slice.122
  212.3 0.0 collective-permute-done.2
  212.3 1.2 collective-permute-done.3
  213.5 0.5 fusion.11
  214.1 0.6 fusion.7
  214.7 1.6 pad_maximum_fusion.1
  216.3 0.8 slice.123
  217.1 3.7 %pad_maximum_fusion.2 = f32[4,8,8,8,8,8]{2,1,0,5,4,3:T(8,128)} fusion(f32[4,8,8,8,8,1]{2,1,0,5,4,3:T(8,128)S(1)} %get-tuple-element.23, f32[4,8,8,8,8,6]{2,1,0,5,4,3:T(8,128)S(1)} %slice.123, f32[4,8,8,8,8,1]{2,1,0,5,4,3:T(8,128)S(1)} %get-tuple-element.22), kind=kLoop, calls=%fused_computation.5 | loop fusion | flops 262144 | bytes 1048576 | tf_op jit(solution)/shard_map/concatenate | solution.py:59
  220.8 5.9 %copy.420 = f32[4,8,8,512]{3,2,1,0:T(8,128)} copy(f32[4,8,8,512]{2,1,0,3:T(8,128)} %bitcast.26) | data formatting | bytes 1048576
  (3 shorter events, 0.1 us)
Async XLA Ops:
  17.5 66.2 %all-to-all-start = ((s32[1,8,1024]{2,0,1:T(1,128)}), s32[1,8,1024]{2,0,1:T(1,128)S(1)}, u32[]{:S(2)}, u32[]{:S(2)}) async-start(s32[1,8,1024]{2,0,1:T(1,128)} %bitcast), calls=%async_computation | async-start | bytes 65536 | tf_op jit(solution)/shard_map/all_to_all | solution.py:96
  83.7 10.8 %all-to-all-start.1 = ((f32[4,8,1024]{2,0,1:T(4,128)}), f32[4,8,1024]{2,0,1:T(4,128)S(1)}, u32[]{:S(2)}, u32[]{:S(2)}) async-start(f32[4,8,1024]{2,0,1:T(4,128)} %copy.405), calls=%async_computation.1 | async-start | bytes 262144 | tf_op jit(solution)/shard_map/all_to_all | solution.py:95
  149.7 4.8 %copy-start = (f32[1,256,32]{2,1,0:T(8,128)S(1)}, f32[1,256,32]{2,1,0:T(8,128)}, u32[]{:S(2)}) copy-start(f32[1,256,32]{2,1,0:T(8,128)} %stack.24) | copy-start | bytes 98308
  184.5 10.2 %collective-permute-start = (f32[1,8,8,1,8,8]{2,1,0,5,4,3:T(8,128)S(1)}, f32[1,8,8,1,8,8]{2,1,0,5,4,3:T(8,128)S(1)}, u32[]{:S(2)}, u32[]{:S(2)}) collective-permute-start(f32[1,8,8,1,8,8]{2,1,0,5,4,3:T(8,128)S(1)} %get-tuple-element.30), channel_id=1, source_target_pairs={{0,8},{8,16},{16,24},{1,9},{9,17},{17,25},{2,10},{10,18},{18,26},{... | collective-permute-start | bytes 49160 | tf_op jit(solution)/shard_map/ppermute | solution.py:19
  188.4 12.2 %collective-permute-start.1 = (f32[1,8,8,1,8,8]{2,1,0,5,4,3:T(8,128)S(1)}, f32[1,8,8,1,8,8]{2,1,0,5,4,3:T(8,128)S(1)}, u32[]{:S(2)}, u32[]{:S(2)}) collective-permute-start(f32[1,8,8,1,8,8]{2,1,0,5,4,3:T(8,128)S(1)} %get-tuple-element.31), channel_id=1, source_target_pairs={{8,0},{16,8},{24,16},{9,1},{17,9},{25,17},{10,2},{18,10},{26,18},{... | collective-permute-start | bytes 49160 | tf_op jit(solution)/shard_map/ppermute | solution.py:22
  202.9 9.4 %collective-permute-start.2 = (f32[4,1,8,8,1,8]{2,1,0,5,4,3:T(1,128)S(1)}, f32[4,1,8,8,1,8]{2,1,0,5,4,3:T(1,128)S(1)}, u32[]{:S(2)}, u32[]{:S(2)}) collective-permute-start(f32[4,1,8,8,1,8]{2,1,0,5,4,3:T(1,128)S(1)} %get-tuple-element.26), channel_id=1, source_target_pairs={{0,1},{1,2},{2,3},{3,4},{4,5},{5,6},{6,7},{8,9},{9,10},{10,11},{11... | collective-permute-start | bytes 24584 | tf_op jit(solution)/shard_map/ppermute | solution.py:19
  207.2 6.3 %collective-permute-start.3 = (f32[4,1,8,8,1,8]{2,1,0,5,4,3:T(1,128)S(1)}, f32[4,1,8,8,1,8]{2,1,0,5,4,3:T(1,128)S(1)}, u32[]{:S(2)}, u32[]{:S(2)}) collective-permute-start(f32[4,1,8,8,1,8]{2,1,0,5,4,3:T(1,128)S(1)} %get-tuple-element.27), channel_id=1, source_target_pairs={{1,0},{2,1},{3,2},{4,3},{5,4},{6,5},{7,6},{9,8},{10,9},{11,10},{12... | collective-permute-start | bytes 24584 | tf_op jit(solution)/shard_map/ppermute | solution.py:22
